TPU v7x, 32 devices: a whole 2x2x4 slice. The times are simulated.
32 devices in a mesh: trial: 4 (over x, core), north: 2 (over y), east: 4 (over z).
Axes of the slice: x: 2, y: 2, z: 4, core: 2. Of those that a mesh axis runs over, the one named last changes fastest.
Arguments:
- pair_state: bfloat16 [192, 48, 128], P(('trial', 'north'), 'east'), parts along dimension 0, may hold values from -6 to 6
- in_gain: float32 [128], replicated, may hold values from 0.25 to 1.75
- left_weight: bfloat16 [512, 128], P('trial'), parts along dimension 0, may hold values from -0.5 to 0.5
- right_weight: bfloat16 [512, 128], P('trial'), parts along dimension 0, may hold values from -0.5 to 0.5
- left_gate: bfloat16 [512, 128], P('trial'), parts along dimension 0, may hold values from -0.5 to 0.5
- right_gate: bfloat16 [512, 128], P('trial'), parts along dimension 0, may hold values from -0.5 to 0.5
- mid_gain: float32 [128], replicated, may hold values from 0.25 to 1.75
- out_weight: bfloat16 [512, 128], P('trial'), parts along dimension 0, may hold values from -0.5 to 0.5
- out_gate: bfloat16 [512, 128], P('trial'), parts along dimension 0, may hold values from -0.5 to 0.5
Outputs:
- triangle_out: bfloat16 [192, 48, 128], P(('trial', 'north'), 'east'), parts along dimension 0
There are 4 independent parts, one for each index of `trial`. A program takes and returns all parts, laid end to end along the dimension named above; an argument that names none is the same for every part. Nothing has to cross between parts.
All inputs are finite; a program needn't handle non-finite values.
Results may differ from a plain program's by a relative error of at most 0.015.
Values may be sent and summed in bfloat16 or wider, within the bound.
A program may use at most 64 MiB of HBM per device.

v0:
```python
import jax
import jax.numpy as jnp
from jax import lax
from jax.sharding import PartitionSpec as P


def norm_channels(values, channel_gain):
    centred = values - jnp.mean(values, axis=-1, keepdims=True)
    return (
        centred
        * lax.rsqrt(jnp.mean(centred * centred, axis=-1, keepdims=True) + 1e-05)
        * channel_gain
    )


def make_factors(pair_in, in_gain, left_weight, right_weight, left_gate, right_gate):
    ready = norm_channels(pair_in.astype(jnp.float32), in_gain).astype(jnp.bfloat16)
    ready = lax.optimization_barrier(ready)
    left = jnp.einsum("ijc,cd->ijd", ready, left_weight, preferred_element_type=jnp.float32)
    left = left * jax.nn.sigmoid(
        jnp.einsum("ijc,cd->ijd", ready, left_gate, preferred_element_type=jnp.float32)
    )
    right = jnp.einsum("ijc,cd->ijd", ready, right_weight, preferred_element_type=jnp.float32)
    right = right * jax.nn.sigmoid(
        jnp.einsum("ijc,cd->ijd", ready, right_gate, preferred_element_type=jnp.float32)
    )
    return (ready, left.astype(jnp.bfloat16), right.astype(jnp.bfloat16))


def to_pair(mixed, ready, mid_gain, out_weight, out_gate):
    scaled = norm_channels(mixed.astype(jnp.float32), mid_gain).astype(jnp.bfloat16)
    scaled = lax.optimization_barrier(scaled)
    gate = jax.nn.sigmoid(
        jnp.einsum("ijc,cd->ijd", ready, out_gate, preferred_element_type=jnp.float32)
    )
    return (
        jnp.einsum("ijd,dc->ijc", scaled, out_weight, preferred_element_type=jnp.float32) * gate
    ).astype(jnp.bfloat16)


def local(
    pair_state,
    in_gain,
    left_weight,
    right_weight,
    left_gate,
    right_gate,
    mid_gain,
    out_weight,
    out_gate,
):
    ready, left, right = make_factors(
        pair_state, in_gain, left_weight, right_weight, left_gate, right_gate
    )
    count = pair_state.shape[1] * lax.axis_size("east")
    left_lines, right_lines = (
        lax.all_to_all(left, "east", split_axis=2, concat_axis=1, tiled=True),
        lax.all_to_all(right, "east", split_axis=2, concat_axis=1, tiled=True),
    )
    strip = jnp.einsum(
        "ikd,jkd->ijd",
        left_lines,
        lax.all_gather(right_lines, "north", axis=0, tiled=True),
        preferred_element_type=jnp.float32,
    )
    strip = (strip * count ** (-0.5)).astype(jnp.bfloat16)
    mixed = lax.all_to_all(strip, "east", split_axis=1, concat_axis=2, tiled=True)
    return to_pair(mixed, ready, mid_gain, out_weight, out_gate)


def solution(mesh):
    return jax.shard_map(
        local,
        mesh=mesh,
        in_specs=(
            P(("trial", "north"), "east", None),
            P(),
            P("trial", None),
            P("trial", None),
            P("trial", None),
            P("trial", None),
            P(),
            P("trial", None),
            P("trial", None),
        ),
        out_specs=P(("trial", "north"), "east", None),
        check_vma=False,
    )
```

profile of v0, /device:TPU:0, one launch (start us, length us, event | category | flops | bytes accessed | tf_op | source)
XLA Modules:
  0.0 44.6 jit_solution(821063206014544712)
XLA Ops:
  0.0 1.1 %convert_reduce_fusion = f32[24,12]{0,1:T(8,128)S(1)} fusion(bf16[24,12,128]{2,0,1:T(8,128)(2,1)} %param.9), kind=kLoop, calls=%fused_computation.25 | loop fusion | flops 73440 | bytes 74880 | tf_op jit(solution)/shard_map/reduce_sum | solution.py:8
  1.3 0.6 %copy-done.4 = f32[128]{0:T(128)S(1)} copy-done((f32[128]{0:T(128)S(1)}, f32[128]{0:T(128)}, u32[]{:S(2)}) %copy-start.4) | copy-done | bytes 536
  2.3 0.6 %copy-done.6 = bf16[128,128]{1,0:T(8,128)(2,1)S(1)} copy-done((bf16[128,128]{1,0:T(8,128)(2,1)S(1)}, bf16[128,128]{1,0:T(8,128)(2,1)}, u32[]{:S(2)}) %copy-start.6) | copy-done | bytes 32792
  3.1 0.4 copy.34
  3.5 1.1 %reshape.41 = bf16[4,2,4608]{2,1,0:T(2,128)(2,1)} reshape(bf16[128,12,24]{2,1,0:T(8,128)(2,1)S(1)} %bitcast.55) | data formatting | bytes 147456
  4.7 6.5 %all-to-all-start = ((bf16[4,2,4608]{2,1,0:T(2,128)(2,1)}), bf16[4,2,4608]{2,1,0:T(2,128)(2,1)S(1)}, u32[]{:S(2)}, u32[]{:S(2)}) async-start(bf16[4,2,4608]{2,1,0:T(2,128)(2,1)} %reshape.41), calls=%async_computation | async-start | bytes 147456 | tf_op jit(solution)/shard_map/all_to_all | solution.py:58
  11.3 0.6 %copy-done.7 = bf16[128,128]{1,0:T(8,128)(2,1)S(1)} copy-done((bf16[128,128]{1,0:T(8,128)(2,1)S(1)}, bf16[128,128]{1,0:T(8,128)(2,1)}, u32[]{:S(2)}) %copy-start.7) | copy-done | bytes 32792
  12.1 0.4 copy.37
  12.5 1.1 %reshape.43 = bf16[4,2,4608]{2,1,0:T(2,128)(2,1)} reshape(bf16[128,12,24]{2,1,0:T(8,128)(2,1)S(1)} %bitcast.56) | data formatting | bytes 147456
  13.7 3.2 %all-to-all-done = bf16[4,2,4608]{2,1,0:T(2,128)(2,1)S(1)} async-done(((bf16[4,2,4608]{2,1,0:T(2,128)(2,1)}), bf16[4,2,4608]{2,1,0:T(2,128)(2,1)S(1)}, u32[]{:S(2)}, u32[]{:S(2)}) %all-to-all-start) | async-done | bytes 73760 | tf_op jit(solution)/shard_map/all_to_all | solution.py:58
  16.9 3.3 %all-to-all-start.1 = ((bf16[4,2,4608]{2,1,0:T(2,128)(2,1)}), bf16[4,2,4608]{2,1,0:T(2,128)(2,1)S(1)}, u32[]{:S(2)}, u32[]{:S(2)}) async-start(bf16[4,2,4608]{2,1,0:T(2,128)(2,1)} %reshape.43), calls=%async_computation.1 | async-start | bytes 147456 | tf_op jit(solution)/shard_map/all_to_all | solution.py:57
  20.2 0.6 %reshape.42 = bf16[128,12,24]{2,1,0:T(8,128)(2,1)S(1)} reshape(bf16[4,2,4608]{2,1,0:T(2,128)(2,1)S(1)} %all-to-all-done) | data formatting | bytes 147456
  20.8 0.4 copy.35
  21.5 6.3 %all_gather.3 = bf16[48,48,32]{1,0,2:T(8,128)(2,1)S(1)} all-gather(bf16[24,48,32]{1,0,2:T(8,128)(2,1)S(1)} %copy.36), channel_id=1, replica_groups=mesh['trial'=4,'north'=2,'east'=4] {'north'}, dimensions={0}, use_global_device_ids=true | all-gather | bytes 221184 | tf_op jit(solution)/shard_map/all_gather | solution.py:63
  27.8 0.6 %reshape.44 = bf16[128,12,24]{2,1,0:T(8,128)(2,1)S(1)} reshape(bf16[4,2,4608]{2,1,0:T(2,128)(2,1)S(1)} %all-to-all-done.1) | data formatting | bytes 147456
  28.4 0.4 copy.38
  29.1 0.3 fusion.1
  29.9 10.6 %all_to_all.45 = bf16[4,2,4608]{2,1,0:T(2,128)(2,1)S(1)} all-to-all(bf16[4,2,4608]{2,1,0:T(2,128)(2,1)S(1)} %reshape.45), channel_id=1, replica_groups=mesh['trial'=4,'north'=2,'east'=4] {'east'}, dimensions={0} | all-to-all | bytes 147456 | tf_op jit(solution)/shard_map/all_to_all | solution.py:67
  41.2 0.4 copy.41
  41.6 0.3 reshape.32
  41.9 0.4 copy-done.5
  42.4 0.6 %copy-done.3 = bf16[128,128]{1,0:T(8,128)(2,1)S(1)} copy-done((bf16[128,128]{1,0:T(8,128)(2,1)S(1)}, bf16[128,128]{1,0:T(8,128)(2,1)}, u32[]{:S(2)}) %copy-start.3) | copy-done | bytes 32792
  43.2 0.6 %copy-done.8 = bf16[128,128]{1,0:T(8,128)(2,1)S(1)} copy-done((bf16[128,128]{1,0:T(8,128)(2,1)S(1)}, bf16[128,128]{1,0:T(8,128)(2,1)}, u32[]{:S(2)}) %copy-start.8) | copy-done | bytes 32792
  43.7 0.8 %fusion.14 = bf16[24,12,128]{2,0,1:T(8,128)(2,1)} fusion(f32[24,12,128]{2,0,1:T(8,128)S(1)} %fusion.24, bf16[24,12,128]{2,0,1:T(8,128)(2,1)S(1)} %fusion.22, bf16[128,128]{1,0:T(8,128)(2,1)S(1)} %copy-done.8), kind=kOutput, calls=%fused_computation.18 | convolution fusion | flops 9621504 | bytes 327680 | tf_op jit(solution)/shard_map/ijc,cd->ijd/dot_general | solution.py:34
  (33 shorter events, 3.0 us)
Async XLA Ops:
  0.0 2.1 %copy-start = (bf16[128,128]{1,0:T(8,128)(2,1)S(1)}, bf16[128,128]{1,0:T(8,128)(2,1)}, u32[]{:S(2)}) copy-start(bf16[128,128]{1,0:T(8,128)(2,1)} %param.12) | copy-start | bytes 98308
  0.0 1.1 %copy-start.1 = (bf16[24,12,128]{2,0,1:T(8,128)(2,1)S(1)}, bf16[24,12,128]{2,0,1:T(8,128)(2,1)}, u32[]{:S(2)}) copy-start(bf16[24,12,128]{2,0,1:T(8,128)(2,1)} %param.9) | copy-start | bytes 221188
  1.3 0.7 %copy-start.4 = (f32[128]{0:T(128)S(1)}, f32[128]{0:T(128)}, u32[]{:S(2)}) copy-start(f32[128]{0:T(128)} %param.10) | copy-start | bytes 1540
  2.1 0.8 %copy-start.6 = (bf16[128,128]{1,0:T(8,128)(2,1)S(1)}, bf16[128,128]{1,0:T(8,128)(2,1)}, u32[]{:S(2)}) copy-start(bf16[128,128]{1,0:T(8,128)(2,1)} %param.14) | copy-start | bytes 98308
  4.7 6.5 %copy-start.2 = (bf16[128,128]{1,0:T(8,128)(2,1)S(1)}, bf16[128,128]{1,0:T(8,128)(2,1)}, u32[]{:S(2)}) copy-start(bf16[128,128]{1,0:T(8,128)(2,1)} %param.11) | copy-start | bytes 98308
  4.7 12.2 %all-to-all-start = ((bf16[4,2,4608]{2,1,0:T(2,128)(2,1)}), bf16[4,2,4608]{2,1,0:T(2,128)(2,1)S(1)}, u32[]{:S(2)}, u32[]{:S(2)}) async-start(bf16[4,2,4608]{2,1,0:T(2,128)(2,1)} %reshape.41), calls=%async_computation | async-start | bytes 147456 | tf_op jit(solution)/shard_map/all_to_all | solution.py:58
  11.1 0.8 %copy-start.7 = (bf16[128,128]{1,0:T(8,128)(2,1)S(1)}, bf16[128,128]{1,0:T(8,128)(2,1)}, u32[]{:S(2)}) copy-start(bf16[128,128]{1,0:T(8,128)(2,1)} %param.13) | copy-start | bytes 98308
  16.9 10.9 %all-to-all-start.1 = ((bf16[4,2,4608]{2,1,0:T(2,128)(2,1)}), bf16[4,2,4608]{2,1,0:T(2,128)(2,1)S(1)}, u32[]{:S(2)}, u32[]{:S(2)}) async-start(bf16[4,2,4608]{2,1,0:T(2,128)(2,1)} %reshape.43), calls=%async_computation.1 | async-start | bytes 147456 | tf_op jit(solution)/shard_map/all_to_all | solution.py:57
  41.6 0.7 %copy-start.5 = (f32[128]{0:T(128)S(1)}, f32[128]{0:T(128)}, u32[]{:S(2)}) copy-start(f32[128]{0:T(128)} %param.15) | copy-start | bytes 1540
  42.2 0.8 %copy-start.3 = (bf16[128,128]{1,0:T(8,128)(2,1)S(1)}, bf16[128,128]{1,0:T(8,128)(2,1)}, u32[]{:S(2)}) copy-start(bf16[128,128]{1,0:T(8,128)(2,1)} %param.16) | copy-start | bytes 98308
  43.0 0.8 %copy-start.8 = (bf16[128,128]{1,0:T(8,128)(2,1)S(1)}, bf16[128,128]{1,0:T(8,128)(2,1)}, u32[]{:S(2)}) copy-start(bf16[128,128]{1,0:T(8,128)(2,1)} %param.17) | copy-start | bytes 98308
where the time goes:
time: 45.3 us; the launch traced here: 44.6 us
  blocking collectives  17 us (38%)
  local copies, waits for them, and re-layouts  10.4 us (23%)
  starting transfers between devices  9.77 us (22%)
  waiting for transfers between devices  3.24 us (7%)
  matrix products  2.02 us (4%)
  other arithmetic  1.96 us (4%)
    all_to_all x1, blocking collectives, local(): lax.all_to_all(strip, 'east', split_axis=1, concat_axis=2, tiled=True)  10.6 us
    unnamed x24, local copies, waits for them, and re-layouts  7.31 us
    all_to_all x1, starting transfers between devices, local(): lax.all_to_all(right, 'east', split_axis=2, concat_axis=1, tiled=True)  6.48 us
    all_gather x1, blocking collectives, local(): lax.all_gather(right_lines, 'north', axis=0, tiled=True)  6.34 us
    all_to_all x1, starting transfers between devices, local(): lax.all_to_all(left, 'east', split_axis=2, concat_axis=1, tiled=True)  3.29 us
    all_to_all x1, waiting for transfers between devices, local(): lax.all_to_all(right, 'east', split_axis=2, concat_axis=1, tiled=True)  3.23 us
    reduce_sum x2, other arithmetic, norm_channels(): centred = values - jnp.mean(values, axis=-1, keepdims=True)  1.19 us
  transfers between devices with their start and end apart: 2, of which 1 were waited for; matrix products, arithmetic and copies ran while one was open for 7% of the time, Pallas kernels for 0%

commit v1 on v0

--- a/solution.py
+++ b/solution.py
@@ -2,6 +2,18 @@
 import jax.numpy as jnp
 from jax import lax
 from jax.sharding import PartitionSpec as P
+
+
+def split_up(x, dim, count):
+    shape = x.shape
+    parts = x.reshape(*shape[:dim], count, shape[dim] // count, *shape[dim + 1 :])
+    return jnp.moveaxis(parts, dim, 0)
+
+
+def joined_along(blocks, dim):
+    shape = list(blocks.shape[1:])
+    shape[dim] *= blocks.shape[0]
+    return jnp.moveaxis(blocks, 0, dim).reshape(shape)
 
 
 def norm_channels(values, channel_gain):
@@ -64,7 +76,14 @@
         preferred_element_type=jnp.float32,
     )
     strip = (strip * count ** (-0.5)).astype(jnp.bfloat16)
-    mixed = lax.all_to_all(strip, "east", split_axis=1, concat_axis=2, tiled=True)
+    size, mine = (lax.axis_size("east"), lax.axis_index("east"))
+    tiles = split_up(strip, 1, size)
+    finished = [tiles[mine]]
+    for step in range(1, size):
+        sent = tiles[(mine + step) % size]
+        finished.append(lax.ppermute(sent, "east", [(i, (i + step) % size) for i in range(size)]))
+    tiles = jnp.stack(finished)[(mine - jnp.arange(size)) % size]
+    mixed = joined_along(tiles, 2)
     return to_pair(mixed, ready, mid_gain, out_weight, out_gate)
 
 

time: 45.3 us -> 43.7 us (0.965)
  blocking collectives: 17 us -> 6.34 us
  starting transfers between devices: 9.77 us -> 15.6 us
  waiting for transfers between devices: 3.24 us -> 6.07 us
    all_to_all x1 -> x0, blocking collectives: 10.6 us -> none  [local(): lax.all_to_all(strip, 'east', split_axis=1, concat_axis=2, tiled=True)]
    ppermute x0 -> x3, starting transfers between devices: none -> 5.86 us  [local(): lax.ppermute(sent, 'east', [(i, (i + step) % size) for i in range(size)])]
    ppermute x0 -> x3, waiting for transfers between devices: none -> 2.89 us  [local(): lax.ppermute(sent, 'east', [(i, (i + step) % size) for i in range(size)])]
    gather x0 -> x1, local copies, waits for them, and re-layouts: none -> 0.6 us  [local(): tiles = jnp.stack(finished)[(mine - jnp.arange(size)) % size]]
    unnamed x24 -> x22, local copies, waits for them, and re-layouts: 7.31 us -> 6.87 us
  transfers between devices with their start and end apart: 2 -> 5, of which waited for: 1 -> 4; matrix products, arithmetic and copies ran while one was open for 7% -> 7% of each run, Pallas kernels for 0% -> 0%
where the time goes in v1:
time: 43.7 us; the launch traced here: 43 us
  starting transfers between devices  15.6 us (36%)
  local copies, waits for them, and re-layouts  10.6 us (24%)
  blocking collectives  6.34 us (15%)
  waiting for transfers between devices  6.07 us (14%)
  other arithmetic  2.06 us (5%)
  matrix products  2.02 us (5%)
    unnamed x22, local copies, waits for them, and re-layouts  6.87 us
    all_to_all x1, starting transfers between devices, local(): lax.all_to_all(right, 'east', split_axis=2, concat_axis=1, tiled=True)  6.48 us
    all_gather x1, blocking collectives, local(): lax.all_gather(right_lines, 'north', axis=0, tiled=True)  6.34 us
    ppermute x3, starting transfers between devices, local(): lax.ppermute(sent, 'east', [(i, (i + step) % size) for i in range(size)])  5.86 us
    all_to_all x1, starting transfers between devices, local(): lax.all_to_all(left, 'east', split_axis=2, concat_axis=1, tiled=True)  3.29 us
    all_to_all x1, waiting for transfers between devices, local(): lax.all_to_all(right, 'east', split_axis=2, concat_axis=1, tiled=True)  3.18 us
    ppermute x3, waiting for transfers between devices, local(): lax.ppermute(sent, 'east', [(i, (i + step) % size) for i in range(size)])  2.89 us
    reduce_sum x2, other arithmetic, norm_channels(): centred = values - jnp.mean(values, axis=-1, keepdims=True)  1.19 us
  transfers between devices with their start and end apart: 5, of which 4 were waited for; matrix products, arithmetic and copies ran while one was open for 7% of the time, Pallas kernels for 0%

profile of v1, /device:TPU:0, one launch (start us, length us, event | category | flops | bytes accessed | tf_op | source)
XLA Modules:
  0.0 43.0 jit_solution(16770071728931304289)
XLA Ops:
  0.0 1.1 %convert_reduce_fusion = f32[24,12]{0,1:T(8,128)S(1)} fusion(bf16[24,12,128]{2,0,1:T(8,128)(2,1)} %param.9), kind=kLoop, calls=%fused_computation.27 | loop fusion | flops 73440 | bytes 74880 | tf_op jit(solution)/shard_map/reduce_sum | solution.py:20
  1.3 0.6 %copy-done.4 = f32[128]{0:T(128)S(1)} copy-done((f32[128]{0:T(128)S(1)}, f32[128]{0:T(128)}, u32[]{:S(2)}) %copy-start.4) | copy-done | bytes 536
  2.3 0.6 %copy-done.6 = bf16[128,128]{1,0:T(8,128)(2,1)S(1)} copy-done((bf16[128,128]{1,0:T(8,128)(2,1)S(1)}, bf16[128,128]{1,0:T(8,128)(2,1)}, u32[]{:S(2)}) %copy-start.6) | copy-done | bytes 32792
  3.1 0.4 copy.23
  3.5 1.1 %reshape.104 = bf16[4,2,4608]{2,1,0:T(2,128)(2,1)} reshape(bf16[128,12,24]{2,1,0:T(8,128)(2,1)S(1)} %bitcast.62) | data formatting | bytes 147456
  4.7 6.5 %all-to-all-start = ((bf16[4,2,4608]{2,1,0:T(2,128)(2,1)}), bf16[4,2,4608]{2,1,0:T(2,128)(2,1)S(1)}, u32[]{:S(2)}, u32[]{:S(2)}) async-start(bf16[4,2,4608]{2,1,0:T(2,128)(2,1)} %reshape.104), calls=%async_computation | async-start | bytes 147456 | tf_op jit(solution)/shard_map/all_to_all | solution.py:70
  11.3 0.6 %copy-done.7 = bf16[128,128]{1,0:T(8,128)(2,1)S(1)} copy-done((bf16[128,128]{1,0:T(8,128)(2,1)S(1)}, bf16[128,128]{1,0:T(8,128)(2,1)}, u32[]{:S(2)}) %copy-start.7) | copy-done | bytes 32792
  12.1 0.4 copy.26
  12.6 1.1 %reshape.106 = bf16[4,2,4608]{2,1,0:T(2,128)(2,1)} reshape(bf16[128,12,24]{2,1,0:T(8,128)(2,1)S(1)} %bitcast.63) | data formatting | bytes 147456
  13.7 3.2 %all-to-all-done = bf16[4,2,4608]{2,1,0:T(2,128)(2,1)S(1)} async-done(((bf16[4,2,4608]{2,1,0:T(2,128)(2,1)}), bf16[4,2,4608]{2,1,0:T(2,128)(2,1)S(1)}, u32[]{:S(2)}, u32[]{:S(2)}) %all-to-all-start) | async-done | bytes 73760 | tf_op jit(solution)/shard_map/all_to_all | solution.py:70
  16.9 3.3 %all-to-all-start.1 = ((bf16[4,2,4608]{2,1,0:T(2,128)(2,1)}), bf16[4,2,4608]{2,1,0:T(2,128)(2,1)S(1)}, u32[]{:S(2)}, u32[]{:S(2)}) async-start(bf16[4,2,4608]{2,1,0:T(2,128)(2,1)} %reshape.106), calls=%async_computation.1 | async-start | bytes 147456 | tf_op jit(solution)/shard_map/all_to_all | solution.py:69
  20.2 0.6 %reshape.105 = bf16[128,12,24]{2,1,0:T(8,128)(2,1)S(1)} reshape(bf16[4,2,4608]{2,1,0:T(2,128)(2,1)S(1)} %all-to-all-done) | data formatting | bytes 147456
  21.5 6.3 %all_gather.3 = bf16[48,48,32]{1,0,2:T(8,128)(2,1)S(1)} all-gather(bf16[24,48,32]{1,0,2:T(8,128)(2,1)S(1)} %copy.25), channel_id=1, replica_groups=mesh['trial'=4,'north'=2,'east'=4] {'north'}, dimensions={0}, use_global_device_ids=true | all-gather | bytes 221184 | tf_op jit(solution)/shard_map/all_gather | solution.py:75
  27.8 0.6 %reshape.107 = bf16[128,12,24]{2,1,0:T(8,128)(2,1)S(1)} reshape(bf16[4,2,4608]{2,1,0:T(2,128)(2,1)S(1)} %all-to-all-done.1) | data formatting | bytes 147456
  28.4 0.4 copy.27
  29.7 2.0 %collective-permute-start = (bf16[24,12,32]{2,0,1:T(8,128)(2,1)S(1)}, bf16[24,12,32]{2,0,1:T(8,128)(2,1)S(1)}, u32[]{:S(2)}, u32[]{:S(2)}) collective-permute-start(bf16[24,12,32]{2,0,1:T(8,128)(2,1)S(1)} %get-tuple-element.8), channel_id=1, source_target_pairs={{0,1},{1,2},{2,3},{3,0},{4,5},{5,6},{6,7},{7,4},{8,9},{9,10},{10,1... | collective-permute-start | bytes 55304 | tf_op jit(solution)/shard_map/ppermute | solution.py:84
  31.7 2.4 %collective-permute-start.1 = (bf16[24,12,32]{2,0,1:T(8,128)(2,1)S(1)}, bf16[24,12,32]{2,0,1:T(8,128)(2,1)S(1)}, u32[]{:S(2)}, u32[]{:S(2)}) collective-permute-start(bf16[24,12,32]{2,0,1:T(8,128)(2,1)S(1)} %get-tuple-element.7), channel_id=1, source_target_pairs={{0,2},{1,3},{2,0},{3,1},{4,6},{5,7},{6,4},{7,5},{8,10},{9,11},{10,... | collective-permute-start | bytes 55304 | tf_op jit(solution)/shard_map/ppermute | solution.py:84
  34.1 1.5 %collective-permute-start.2 = (bf16[24,12,32]{2,0,1:T(8,128)(2,1)S(1)}, bf16[24,12,32]{2,0,1:T(8,128)(2,1)S(1)}, u32[]{:S(2)}, u32[]{:S(2)}) collective-permute-start(bf16[24,12,32]{2,0,1:T(8,128)(2,1)S(1)} %get-tuple-element.6), channel_id=1, source_target_pairs={{0,3},{1,0},{2,1},{3,2},{4,7},{5,4},{6,5},{7,6},{8,11},{9,8},{10,9... | collective-permute-start | bytes 55304 | tf_op jit(solution)/shard_map/ppermute | solution.py:84
  35.9 1.1 %collective-permute-done.1 = bf16[24,12,32]{2,0,1:T(8,128)(2,1)S(1)} collective-permute-done((bf16[24,12,32]{2,0,1:T(8,128)(2,1)S(1)}, bf16[24,12,32]{2,0,1:T(8,128)(2,1)S(1)}, u32[]{:S(2)}, u32[]{:S(2)}) %collective-permute-start.1) | collective-permute-done | bytes 18464 | tf_op jit(solution)/shard_map/ppermute | solution.py:84
  37.0 1.5 %collective-permute-done.2 = bf16[24,12,32]{2,0,1:T(8,128)(2,1)S(1)} collective-permute-done((bf16[24,12,32]{2,0,1:T(8,128)(2,1)S(1)}, bf16[24,12,32]{2,0,1:T(8,128)(2,1)S(1)}, u32[]{:S(2)}, u32[]{:S(2)}) %collective-permute-start.2) | collective-permute-done | bytes 18464 | tf_op jit(solution)/shard_map/ppermute | solution.py:84
  38.6 0.6 %gather_fusion = bf16[4,24,12,32]{3,1,2,0:T(8,128)(2,1)S(1)} fusion(bf16[4,24,12,32]{3,1,2,0:T(8,128)(2,1)S(1)} %pad_maximum_fusion, s32[1024]{0:T(1024)S(1)} %pad_clamp_fusion), kind=kCustom, calls=%fused_computation | custom fusion | bytes 147472 | tf_op jit(solution)/shard_map/gather | solution.py:85
  40.8 0.6 %copy-done.3 = bf16[128,128]{1,0:T(8,128)(2,1)S(1)} copy-done((bf16[128,128]{1,0:T(8,128)(2,1)S(1)}, bf16[128,128]{1,0:T(8,128)(2,1)}, u32[]{:S(2)}) %copy-start.3) | copy-done | bytes 32792
  41.6 0.6 %copy-done.8 = bf16[128,128]{1,0:T(8,128)(2,1)S(1)} copy-done((bf16[128,128]{1,0:T(8,128)(2,1)S(1)}, bf16[128,128]{1,0:T(8,128)(2,1)}, u32[]{:S(2)}) %copy-start.8) | copy-done | bytes 32792
  42.2 0.8 %fusion.14 = bf16[24,12,128]{2,0,1:T(8,128)(2,1)} fusion(f32[24,12,128]{2,0,1:T(8,128)S(1)} %fusion.24, bf16[24,12,128]{2,0,1:T(8,128)(2,1)S(1)} %fusion.22, bf16[128,128]{1,0:T(8,128)(2,1)S(1)} %copy-done.8), kind=kOutput, calls=%fused_computation.19 | convolution fusion | flops 9621504 | bytes 327680 | tf_op jit(solution)/shard_map/ijc,cd->ijd/dot_general | solution.py:46
  (41 shorter events, 4.8 us)
Async XLA Ops:
  0.0 2.1 %copy-start = (bf16[128,128]{1,0:T(8,128)(2,1)S(1)}, bf16[128,128]{1,0:T(8,128)(2,1)}, u32[]{:S(2)}) copy-start(bf16[128,128]{1,0:T(8,128)(2,1)} %param.12) | copy-start | bytes 98308
  0.0 1.1 %copy-start.1 = (bf16[24,12,128]{2,0,1:T(8,128)(2,1)S(1)}, bf16[24,12,128]{2,0,1:T(8,128)(2,1)}, u32[]{:S(2)}) copy-start(bf16[24,12,128]{2,0,1:T(8,128)(2,1)} %param.9) | copy-start | bytes 221188
  1.3 0.7 %copy-start.4 = (f32[128]{0:T(128)S(1)}, f32[128]{0:T(128)}, u32[]{:S(2)}) copy-start(f32[128]{0:T(128)} %param.10) | copy-start | bytes 1540
  2.1 0.8 %copy-start.6 = (bf16[128,128]{1,0:T(8,128)(2,1)S(1)}, bf16[128,128]{1,0:T(8,128)(2,1)}, u32[]{:S(2)}) copy-start(bf16[128,128]{1,0:T(8,128)(2,1)} %param.14) | copy-start | bytes 98308
  4.7 6.5 %copy-start.2 = (bf16[128,128]{1,0:T(8,128)(2,1)S(1)}, bf16[128,128]{1,0:T(8,128)(2,1)}, u32[]{:S(2)}) copy-start(bf16[128,128]{1,0:T(8,128)(2,1)} %param.11) | copy-start | bytes 98308
  4.7 12.2 %all-to-all-start = ((bf16[4,2,4608]{2,1,0:T(2,128)(2,1)}), bf16[4,2,4608]{2,1,0:T(2,128)(2,1)S(1)}, u32[]{:S(2)}, u32[]{:S(2)}) async-start(bf16[4,2,4608]{2,1,0:T(2,128)(2,1)} %reshape.104), calls=%async_computation | async-start | bytes 147456 | tf_op jit(solution)/shard_map/all_to_all | solution.py:70
  11.1 0.8 %copy-start.7 = (bf16[128,128]{1,0:T(8,128)(2,1)S(1)}, bf16[128,128]{1,0:T(8,128)(2,1)}, u32[]{:S(2)}) copy-start(bf16[128,128]{1,0:T(8,128)(2,1)} %param.13) | copy-start | bytes 98308
  16.9 10.9 %all-to-all-start.1 = ((bf16[4,2,4608]{2,1,0:T(2,128)(2,1)}), bf16[4,2,4608]{2,1,0:T(2,128)(2,1)S(1)}, u32[]{:S(2)}, u32[]{:S(2)}) async-start(bf16[4,2,4608]{2,1,0:T(2,128)(2,1)} %reshape.106), calls=%async_computation.1 | async-start | bytes 147456 | tf_op jit(solution)/shard_map/all_to_all | solution.py:69
  29.7 6.2 %collective-permute-start = (bf16[24,12,32]{2,0,1:T(8,128)(2,1)S(1)}, bf16[24,12,32]{2,0,1:T(8,128)(2,1)S(1)}, u32[]{:S(2)}, u32[]{:S(2)}) collective-permute-start(bf16[24,12,32]{2,0,1:T(8,128)(2,1)S(1)} %get-tuple-element.8), channel_id=1, source_target_pairs={{0,1},{1,2},{2,3},{3,0},{4,5},{5,6},{6,7},{7,4},{8,9},{9,10},{10,1... | collective-permute-start | bytes 55304 | tf_op jit(solution)/shard_map/ppermute | solution.py:84
  31.7 5.3 %collective-permute-start.1 = (bf16[24,12,32]{2,0,1:T(8,128)(2,1)S(1)}, bf16[24,12,32]{2,0,1:T(8,128)(2,1)S(1)}, u32[]{:S(2)}, u32[]{:S(2)}) collective-permute-start(bf16[24,12,32]{2,0,1:T(8,128)(2,1)S(1)} %get-tuple-element.7), channel_id=1, source_target_pairs={{0,2},{1,3},{2,0},{3,1},{4,6},{5,7},{6,4},{7,5},{8,10},{9,11},{10,... | collective-permute-start | bytes 55304 | tf_op jit(solution)/shard_map/ppermute | solution.py:84
  34.1 4.4 %collective-permute-start.2 = (bf16[24,12,32]{2,0,1:T(8,128)(2,1)S(1)}, bf16[24,12,32]{2,0,1:T(8,128)(2,1)S(1)}, u32[]{:S(2)}, u32[]{:S(2)}) collective-permute-start(bf16[24,12,32]{2,0,1:T(8,128)(2,1)S(1)} %get-tuple-element.6), channel_id=1, source_target_pairs={{0,3},{1,0},{2,1},{3,2},{4,7},{5,4},{6,5},{7,6},{8,11},{9,8},{10,9... | collective-permute-start | bytes 55304 | tf_op jit(solution)/shard_map/ppermute | solution.py:84
  40.0 0.7 %copy-start.5 = (f32[128]{0:T(128)S(1)}, f32[128]{0:T(128)}, u32[]{:S(2)}) copy-start(f32[128]{0:T(128)} %param.15) | copy-start | bytes 1540
  40.7 0.8 %copy-start.3 = (bf16[128,128]{1,0:T(8,128)(2,1)S(1)}, bf16[128,128]{1,0:T(8,128)(2,1)}, u32[]{:S(2)}) copy-start(bf16[128,128]{1,0:T(8,128)(2,1)} %param.16) | copy-start | bytes 98308
  41.4 0.8 %copy-start.8 = (bf16[128,128]{1,0:T(8,128)(2,1)S(1)}, bf16[128,128]{1,0:T(8,128)(2,1)}, u32[]{:S(2)}) copy-start(bf16[128,128]{1,0:T(8,128)(2,1)} %param.17) | copy-start | bytes 98308
